TPU v7x, 512 devices: a whole 4x8x8 slice. The times are simulated.
512 devices in a mesh: sub: 8 (over y), row: 4 (over x_hi, core), col: 16 (over z, x_lo).
Axes of the slice: x: 4 (x_hi: 2, x_lo: 2; x = x_hi * 2 + x_lo), y: 8, z: 8, core: 2. Of those that a mesh axis runs over, the one named last changes fastest.
Arguments:
- factor_window: bfloat16 [8, 8192, 1024], P('sub', ('row', 'col'))
- right_sides: bfloat16 [8, 8192, 2048], P('sub', 'row', 'col'), may hold values from -1.1953125 to 1.1953125
- first_block: int32 [8, 8], P('sub'), may hold values from 0 to 4
- tile_map: int32 [8, 8], P('sub'), may hold values from 0 to 15, as said below
- interface_block: float32 [4096, 4096], P(('sub', 'row'), 'col'), may hold values from -6 to 6
Outputs:
- updated_sides: bfloat16 [8, 8192, 2048], P('sub', 'row', 'col')
- schur_global: float32 [4096, 4096], P(('sub', 'row'), 'col')
Inputs may be any that keep to these rules, and one draw needn't show every extreme that they name: `tile_map`: the 8 entries of a subdomain are different global tiles.
All inputs are finite; a program needn't handle non-finite values.
Results may differ from a plain program's by a relative error of at most 0.0075.
Values may be sent and summed in bfloat16 or wider, within the bound.
A program may use at most 64 MiB of HBM per device.

v0:
```python
import jax
import jax.numpy as jnp
from jax import lax
from jax.sharding import Mesh
from jax.sharding import PartitionSpec as P

PANEL = 256
BLOCK = 256
STEPS = 4
GTILES = 16
COL = ("col_0", "col_1")
ROW_COL = ("row", "col_0", "col_1")


def laid_out(parts, dim):
    parts = jnp.moveaxis(parts, 0, dim)
    lengths = parts.shape
    return parts.reshape(*lengths[:dim], lengths[dim] * lengths[dim + 1], *lengths[dim + 2 :])


def copy_for_each(shard, axis):
    length = lax.axis_size(axis)
    return lax.all_to_all(
        jnp.broadcast_to(shard[None], (length, *shard.shape)), axis, 0, 0, tiled=True
    )


def collect(shard, axis, dim):
    return laid_out(copy_for_each(shard, axis), dim)


def picked(shard, axis, root):
    return lax.dynamic_index_in_dim(lax.all_gather(shard, axis), root, 0, keepdims=False)


def whole_of(shard, axes, dim):
    for axis in reversed(axes):
        shard = lax.all_gather(shard, axis, axis=dim, tiled=True)
    return shard


def split_up(shard, dim, length):
    lengths = shard.shape
    parts = shard.reshape(*lengths[:dim], length, lengths[dim] // length, *lengths[dim + 1 :])
    return jnp.moveaxis(parts, dim, 0)


def summed_on_arrival(shard, axis, dim):
    length = lax.axis_size(axis)
    parts = lax.all_to_all(split_up(shard, dim, length), axis, 0, 0, tiled=True)
    return jnp.sum(parts.astype(jnp.float32), axis=0)


def spread_tiles(columns, tile_map, block_count):
    onehot = (tile_map[0][:, None] == jnp.arange(GTILES, dtype=jnp.int32)[None, :]).astype(
        jnp.bfloat16
    )
    height = columns.shape[0]
    spread = jnp.einsum(
        "qbj,bg->qgj",
        columns.reshape(height, block_count, BLOCK),
        onehot,
        preferred_element_type=jnp.float32,
    )
    return spread.reshape(height, GTILES * BLOCK).astype(jnp.bfloat16)


def local(factor_window, right_sides, first_block, tile_map, interface_block):
    row_count = lax.axis_size("row")
    row_pos = lax.axis_index("row")
    col_pos = lax.axis_index(COL)
    local_factor = factor_window[0]
    local_sides = right_sides[0]
    block_rows = local_sides.shape[0]
    block_cols = local_sides.shape[1]
    block_count = first_block.shape[1]
    row_global = row_pos * block_rows + jnp.arange(block_rows, dtype=jnp.int32)
    col_global = col_pos * block_cols + jnp.arange(block_cols, dtype=jnp.int32)
    col_block = col_global // BLOCK
    block_ids = jnp.arange(block_count, dtype=jnp.int32)
    first_col = jnp.sum(
        jnp.where(col_block[:, None] == block_ids[None, :], first_block[0][None, :], 0), axis=1
    )
    live = (row_global // PANEL)[:, None] >= first_col[None, :]
    current = jnp.where(live, local_sides.astype(jnp.float32), jnp.float32(0.0))
    is_root = row_pos == 0
    pieces = []
    for panel in range(STEPS):
        offset = panel * PANEL
        panel_cols = collect(local_factor[:, offset : offset + PANEL], COL, 0)
        diag_block = panel_cols[offset : offset + PANEL].astype(jnp.float32)
        diag_block = jnp.where(is_root, diag_block, jnp.eye(PANEL, dtype=jnp.float32))
        solved = jax.scipy.linalg.solve_triangular(
            diag_block, current[offset : offset + PANEL], lower=True
        ).astype(jnp.bfloat16)
        solved = picked(solved, "row", 0)
        update = jnp.dot(panel_cols, solved, preferred_element_type=jnp.float32)
        current = jnp.where((row_global >= offset + PANEL)[:, None], current - update, current)
        placed = jnp.where(is_root, solved.astype(jnp.float32), current[offset : offset + PANEL])
        current = current.at[offset : offset + PANEL].set(placed)
        pieces.append(solved)
    updated_sides = current.astype(jnp.bfloat16)[None]
    stacked = jnp.concatenate(pieces, axis=0)
    out_rows = interface_block.shape[0]
    out_cols = interface_block.shape[1]
    whole_columns = whole_of(stacked, COL, 1)
    spread = spread_tiles(whole_columns, tile_map, block_count)
    my_columns = lax.dynamic_slice_in_dim(spread, col_pos * out_cols, out_cols, 1)
    start = jnp.int32(0)
    results = []
    for piece in range(out_rows * lax.axis_size("sub") // out_rows):
        sub_slot = (start + piece * out_rows) // out_rows
        glob_start = (sub_slot * row_count + row_pos) * out_rows
        left = lax.dynamic_slice_in_dim(spread, glob_start, out_rows, 1)
        results.append(
            lax.dot_general(
                left, my_columns, (((0,), (0,)), ((), ())), preferred_element_type=jnp.float32
            )
        )
    summed = summed_on_arrival(jnp.concatenate(results, axis=0).astype(jnp.bfloat16), "sub", 0)
    schur_global = interface_block - summed
    return (updated_sides, schur_global)


def solution(mesh):
    finer = Mesh(
        mesh.devices.reshape(mesh.shape["sub"], mesh.shape["row"], 8, 2),
        ("sub", "row", "col_0", "col_1"),
    )
    placed = (
        P("sub", ROW_COL, None),
        P("sub", "row", COL),
        P("sub", None),
        P("sub", None),
        P(("sub", "row"), COL),
    )
    return jax.shard_map(
        local,
        mesh=finer,
        in_specs=placed,
        out_specs=(P("sub", "row", COL), P(("sub", "row"), COL)),
        check_vma=False,
    )
```

profile of v0, /device:TPU:1, one launch (start us, length us, event | category | flops | bytes accessed | tf_op | source)
XLA Modules:
  0.0 347.8 jit_solution(12843615819082590356)
XLA Ops:
  9.2 11.9 %all-to-all-start = ((bf16[16,128,256]{2,1,0:T(8,128)(2,1)}), bf16[16,128,256]{2,1,0:T(8,128)(2,1)S(1)}, u32[]{:S(2)}, u32[]{:S(2)}) async-start(bf16[16,128,256]{2,1,0:T(8,128)(2,1)} %broadcast_in_dim.85), calls=%async_computation | async-start | bytes 2097152 | tf_op jit(solution)/shard_map/all_to_all | solution.py:23
  21.2 25.4 %all-to-all-done = bf16[16,128,256]{2,1,0:T(8,128)(2,1)S(1)} async-done(((bf16[16,128,256]{2,1,0:T(8,128)(2,1)}), bf16[16,128,256]{2,1,0:T(8,128)(2,1)S(1)}, u32[]{:S(2)}, u32[]{:S(2)}) %all-to-all-start) | async-done | bytes 1048608 | tf_op jit(solution)/shard_map/all_to_all | solution.py:23
  47.7 6.2 %all-to-all-start.1 = ((bf16[16,128,256]{2,1,0:T(8,128)(2,1)}), bf16[16,128,256]{2,1,0:T(8,128)(2,1)S(1)}, u32[]{:S(2)}, u32[]{:S(2)}) async-start(bf16[16,128,256]{2,1,0:T(8,128)(2,1)} %broadcast_in_dim.86), calls=%async_computation.1 | async-start | bytes 2097152 | tf_op jit(solution)/shard_map/all_to_all | solution.py:23
  54.8 2.3 convert_select_fusion
  57.3 3.7 %while.12 = (s32[]{:T(128)}, f32[256,256]{1,0:T(8,128)S(1)}, s32[2,2]{1,0:T(2,128)S(1)}, f32[2,128,128]{2,1,0:T(8,128)S(1)}, s32[]{:T(128)}) while((s32[]{:T(128)}, f32[256,256]{1,0:T(8,128)S(1)}, s32[2,2]{1,0:T(2,128)S(1)}, f32[2,128,128]{2,1,0:T(8,128)S(1)}, s32[]{:T(128)}) %tuple.87), condition=%wide.while_cond.4, body=%wide.while_body.4.sunk | while | flops 2 | bytes 131189 | solution.py:93
  61.0 19.7 %custom-call.6 = f32[2,128,128]{1,2,0:T(8,128)S(1)} custom-call(f32[2,128,128]{2,1,0:T(8,128)S(1)} %get-tuple-element.77), custom_call_target="InvertDiagBlocksLowerTriangular" | custom-call | tf_op jit(solution)/shard_map/jit(_solve_triangular)/triangular_solve | solution.py:93
  81.8 7.5 %all-to-all-start.2 = ((bf16[16,128,256]{2,1,0:T(8,128)(2,1)}), bf16[16,128,256]{2,1,0:T(8,128)(2,1)S(1)}, u32[]{:S(2)}, u32[]{:S(2)}) async-start(bf16[16,128,256]{2,1,0:T(8,128)(2,1)} %broadcast_in_dim.87), calls=%async_computation.2 | async-start | bytes 2097152 | tf_op jit(solution)/shard_map/all_to_all | solution.py:23
  89.4 3.8 %while.13 = (s32[]{:T(128)}, f32[256,256]{1,0:T(8,128)S(1)}, s32[2,2]{1,0:T(2,128)S(1)}, f32[2,128,128]{2,1,0:T(8,128)S(1)}, s32[]{:T(128)}) while((s32[]{:T(128)}, f32[256,256]{1,0:T(8,128)S(1)}, s32[2,2]{1,0:T(2,128)S(1)}, f32[2,128,128]{2,1,0:T(8,128)S(1)}, s32[]{:T(128)}) %tuple.101), condition=%wide.while_cond.4.clone, body=%wide.while_body.4.clone.sunk | while | flops 2 | bytes 131189 | solution.py:93
  95.4 19.7 %custom-call.7 = f32[2,128,128]{1,2,0:T(8,128)S(1)} custom-call(f32[2,128,128]{2,1,0:T(8,128)S(1)} %get-tuple-element.78), custom_call_target="InvertDiagBlocksLowerTriangular" | custom-call | tf_op jit(solution)/shard_map/jit(_solve_triangular)/triangular_solve | solution.py:93
  115.4 9.3 %all-gather = bf16[1024,128]{1,0:T(8,128)(2,1)S(1)} all-gather(bf16[256,128]{1,0:T(8,128)(2,1)S(1)} %maximum_convert_fusion), channel_id=2, replica_groups=mesh['sub'=8,'row'=4,'col_0'=8,'col_1'=2] {'row'}, dimensions={0}, use_global_device_ids=true | all-gather | bytes 327680 | tf_op jit(solution)/shard_map/all_gather | solution.py:33
  124.7 2.1 fusion.1
  127.8 7.8 %all-gather.1 = bf16[1024,128]{1,0:T(8,128)(2,1)} all-gather(bf16[256,128]{1,0:T(8,128)(2,1)S(1)} %maximum_convert_fusion.1), channel_id=3, replica_groups=mesh['sub'=8,'row'=4,'col_0'=8,'col_1'=2] {'row'}, dimensions={0}, use_global_device_ids=true | all-gather | bytes 327680 | tf_op jit(solution)/shard_map/all_gather | solution.py:33
  136.7 7.8 %all-to-all-start.3 = ((bf16[16,128,256]{2,1,0:T(8,128)(2,1)}), bf16[16,128,256]{2,1,0:T(8,128)(2,1)S(1)}, u32[]{:S(2)}, u32[]{:S(2)}) async-start(bf16[16,128,256]{2,1,0:T(8,128)(2,1)} %broadcast_in_dim.88), calls=%async_computation.3 | async-start | bytes 2097152 | tf_op jit(solution)/shard_map/all_to_all | solution.py:23
  145.5 5.2 %while.14 = (s32[]{:T(128)}, f32[256,256]{1,0:T(8,128)S(1)}, s32[2,2]{1,0:T(2,128)S(1)}, f32[2,128,128]{2,1,0:T(8,128)}, s32[]{:T(128)}) while((s32[]{:T(128)}, f32[256,256]{1,0:T(8,128)S(1)}, s32[2,2]{1,0:T(2,128)S(1)}, f32[2,128,128]{2,1,0:T(8,128)}, s32[]{:T(128)}) %tuple.102), condition=%wide.while_cond.4.clone.1, body=%wide.while_body.4.clone.1.sunk | while | flops 2 | bytes 132205 | solution.py:93
  146.1 2.0 bitcast_dynamic-update-slice_fusion.10
  148.7 2.0 bitcast_dynamic-update-slice_fusion.10
  150.7 21.1 %custom-call.8 = f32[2,128,128]{1,2,0:T(8,128)} custom-call(f32[2,128,128]{2,1,0:T(8,128)} %get-tuple-element.79), custom_call_target="InvertDiagBlocksLowerTriangular" | custom-call | tf_op jit(solution)/shard_map/jit(_solve_triangular)/triangular_solve | solution.py:93
  171.8 1.7 fusion.3
  176.8 7.6 %all-gather.2 = bf16[1024,128]{1,0:T(8,128)(2,1)S(1)} all-gather(bf16[256,128]{1,0:T(8,128)(2,1)S(1)} %maximum_convert_fusion.2), channel_id=4, replica_groups=mesh['sub'=8,'row'=4,'col_0'=8,'col_1'=2] {'row'}, dimensions={0}, use_global_device_ids=true | all-gather | bytes 327680 | tf_op jit(solution)/shard_map/all_gather | solution.py:33
  185.0 4.0 %while.15 = (s32[]{:T(128)}, f32[256,256]{1,0:T(8,128)S(1)}, s32[2,2]{1,0:T(2,128)S(1)}, f32[2,128,128]{2,1,0:T(8,128)S(1)}, s32[]{:T(128)}) while((s32[]{:T(128)}, f32[256,256]{1,0:T(8,128)S(1)}, s32[2,2]{1,0:T(2,128)S(1)}, f32[2,128,128]{2,1,0:T(8,128)S(1)}, s32[]{:T(128)}) %tuple.103), condition=%wide.while_cond.4.clone.2, body=%wide.while_body.4.clone.2.sunk | while | flops 2 | bytes 131189 | solution.py:93
  189.0 19.7 %custom-call.9 = f32[2,128,128]{1,2,0:T(8,128)S(1)} custom-call(f32[2,128,128]{2,1,0:T(8,128)S(1)} %get-tuple-element.80), custom_call_target="InvertDiagBlocksLowerTriangular" | custom-call | tf_op jit(solution)/shard_map/jit(_solve_triangular)/triangular_solve | solution.py:93
  209.5 7.4 %all-gather.3 = bf16[1024,128]{1,0:T(8,128)(2,1)S(1)} all-gather(bf16[256,128]{1,0:T(8,128)(2,1)S(1)} %maximum_convert_fusion.3), channel_id=5, replica_groups=mesh['sub'=8,'row'=4,'col_0'=8,'col_1'=2] {'row'}, dimensions={0}, use_global_device_ids=true | all-gather | bytes 327680 | tf_op jit(solution)/shard_map/all_gather | solution.py:33
  217.4 9.0 %all_gather.38 = bf16[1024,256]{1,0:T(8,128)(2,1)} all-gather(bf16[1024,128]{1,0:T(8,128)(2,1)S(1)} %pad_maximum_fusion), channel_id=1, replica_groups=mesh['sub'=8,'row'=4,'col_0'=8,'col_1'=2] {'col_1'}, dimensions={1}, use_global_device_ids=true | all-gather | bytes 786432 | tf_op jit(solution)/shard_map/all_gather | solution.py:38
  226.5 63.3 %all-gather.6.cloned.1.call-done = bf16[1024,2048]{1,0:T(8,128)(2,1)} async-done(((bf16[1024,256]{1,0:T(8,128)(2,1)}), bf16[1024,2048]{1,0:T(8,128)(2,1)}) %all-gather.6.cloned.1.call-update) | async-done | bytes 4194320 | tf_op jit(solution)/shard_map/all_gather | solution.py:38
  289.7 3.7 %copy.19 = bf16[128,8,8,256]{3,2,1,0:T(8,128)(2,1)S(1)} copy(bf16[128,8,8,256]{3,1,2,0:T(8,128)(2,1)} %bitcast.150) | data formatting | bytes 8388608
  293.4 5.2 %convolution_convert_fusion = bf16[16,1024,256]{2,0,1:T(8,128)(2,1)} fusion(bf16[1024,8,256]{2,1,0:T(8,128)(2,1)S(1)} %bitcast.146, s32[8]{0:T(128)S(1)} %bitcast.155), kind=kOutput, calls=%fused_computation.8 | convolution fusion | flops 71303296 | bytes 12582944 | tf_op jit(solution)/shard_map/qbj,bg->qgj/dot_general | solution.py:59
  298.6 12.2 %copy.20 = bf16[128,8,16,256]{3,1,2,0:T(8,128)(2,1)} copy(bf16[128,8,16,256]{3,2,1,0:T(8,128)(2,1)} %bitcast.137) | data formatting | bytes 16777216
  310.8 1.4 fusion.15
  312.3 1.4 fusion.14
  313.7 1.4 fusion.13
  317.9 1.4 fusion.10
  322.2 18.1 %all_to_all.25 = bf16[8,128,256]{2,1,0:T(8,128)(2,1)S(1)} all-to-all(bf16[8,128,256]{2,1,0:T(8,128)(2,1)S(1)} %bitcast.152), channel_id=1, replica_groups=mesh['sub'=8,'row'=4,'col_0'=8,'col_1'=2] {'sub'}, dimensions={0} | all-to-all | bytes 1048576 | tf_op jit(solution)/shard_map/all_to_all | solution.py:50
  (99 shorter events, 34.9 us)
Async XLA Ops:
  9.2 37.3 %all-to-all-start = ((bf16[16,128,256]{2,1,0:T(8,128)(2,1)}), bf16[16,128,256]{2,1,0:T(8,128)(2,1)S(1)}, u32[]{:S(2)}, u32[]{:S(2)}) async-start(bf16[16,128,256]{2,1,0:T(8,128)(2,1)} %broadcast_in_dim.85), calls=%async_computation | async-start | bytes 2097152 | tf_op jit(solution)/shard_map/all_to_all | solution.py:23
  46.5 35.2 %copy-start.1 = (bf16[16,128,256]{2,1,0:T(8,128)(2,1)}, bf16[16,128,256]{2,1,0:T(8,128)(2,1)S(1)}, u32[]{:S(2)}) copy-start(bf16[16,128,256]{2,1,0:T(8,128)(2,1)S(1)} %all-to-all-done) | copy-start | bytes 3145732
  47.7 32.9 %all-to-all-start.1 = ((bf16[16,128,256]{2,1,0:T(8,128)(2,1)}), bf16[16,128,256]{2,1,0:T(8,128)(2,1)S(1)}, u32[]{:S(2)}, u32[]{:S(2)}) async-start(bf16[16,128,256]{2,1,0:T(8,128)(2,1)} %broadcast_in_dim.86), calls=%async_computation.1 | async-start | bytes 2097152 | tf_op jit(solution)/shard_map/all_to_all | solution.py:23
  81.8 53.8 %all-to-all-start.2 = ((bf16[16,128,256]{2,1,0:T(8,128)(2,1)}), bf16[16,128,256]{2,1,0:T(8,128)(2,1)S(1)}, u32[]{:S(2)}, u32[]{:S(2)}) async-start(bf16[16,128,256]{2,1,0:T(8,128)(2,1)} %broadcast_in_dim.87), calls=%async_computation.2 | async-start | bytes 2097152 | tf_op jit(solution)/shard_map/all_to_all | solution.py:23
  124.7 12.0 %copy-start.3 = (bf16[1024,128]{1,0:T(8,128)(2,1)}, bf16[1024,128]{1,0:T(8,128)(2,1)S(1)}, u32[]{:S(2)}) copy-start(bf16[1024,128]{1,0:T(8,128)(2,1)S(1)} %all-gather) | copy-start | bytes 786436
  126.8 1.0 copy-start
  136.7 48.3 %all-to-all-start.3 = ((bf16[16,128,256]{2,1,0:T(8,128)(2,1)}), bf16[16,128,256]{2,1,0:T(8,128)(2,1)S(1)}, u32[]{:S(2)}, u32[]{:S(2)}) async-start(bf16[16,128,256]{2,1,0:T(8,128)(2,1)} %broadcast_in_dim.88), calls=%async_computation.3 | async-start | bytes 2097152 | tf_op jit(solution)/shard_map/all_to_all | solution.py:23
  144.5 72.9 %slice-start = ((bf16[1024,128]{1,0:T(8,128)(2,1)}), bf16[256,128]{1,0:T(8,128)(2,1)S(1)}, s32[]{:S(2)}) async-start(bf16[1024,128]{1,0:T(8,128)(2,1)} %all-gather.1), calls=%async_computation.6 | async-start | bytes 131072 | tf_op jit(solution)/shard_map/jit(dynamic_index_in_dim)/dynamic_slice | solution.py:33
  144.5 72.9 %slice-start.1 = ((bf16[1024,128]{1,0:T(8,128)(2,1)}), bf16[256,128]{1,0:T(8,128)(2,1)S(1)}, s32[]{:S(2)}) async-start(bf16[1024,128]{1,0:T(8,128)(2,1)} %copy-done.3), calls=%async_computation.7 | async-start | bytes 131072 | tf_op jit(solution)/shard_map/jit(dynamic_index_in_dim)/dynamic_slice | solution.py:33
  144.5 145.2 %all-gather.6.cloned.1.call-start = ((), (), s32[]{:S(2)}) async-start(), calls=%async_computation.5 | async-start | bytes 4718592 | tf_op jit(solution)/shard_map/all_gather | solution.py:38
  184.9 108.6 %copy-start.5 = (s32[1,8]{1,0:T(1,128)S(1)}, s32[1,8]{1,0:T(1,128)}, u32[]{:S(2)}) copy-start(s32[1,8]{1,0:T(1,128)} %param.18) | copy-start | bytes 100
  217.4 81.2 %copy-start.2 = (bf16[2048,128]{1,0:T(8,128)(2,1)}, bf16[2048,128]{1,0:T(8,128)(2,1)S(1)}, u32[]{:S(2)}) copy-start(bf16[2048,128]{1,0:T(8,128)(2,1)S(1)} %get-tuple-element.122) | copy-start | bytes 1572868
  310.8 29.5 %copy-start.4 = (f32[128,256]{1,0:T(8,128)S(1)}, f32[128,256]{1,0:T(8,128)}, u32[]{:S(2)}) copy-start(f32[128,256]{1,0:T(8,128)} %param.19) | copy-start | bytes 393220
Sparse Core Ops, SparseCore 0:
  226.6 63.1 all-gather.5
where the time goes:
time: 354 us; the launch traced here: 348 us
  waiting for transfers between devices  88.7 us (25%)
  other arithmetic  85.2 us (24%)
  blocking collectives  59.1 us (17%)
  local copies, waits for them, and re-layouts  38.9 us (11%)
  starting transfers between devices  33.7 us (10%)
  matrix products  27.5 us (8%)
  between operations  14.6 us (4%)
    another operation x9, other arithmetic, local(): jax.scipy.linalg.solve_triangular(diag_block, current[offset:offset + PAN...  80.3 us
    all_gather x1, waiting for transfers between devices, whole_of(): shard = lax.all_gather(shard, axis, axis=dim, tiled=True)  63.3 us
    all_to_all x4, starting transfers between devices, copy_for_each(): lax.all_to_all(jnp.broadcast_to(shard[None], (length, *shard.shape)), axi...  33.5 us
    all_gather x4, blocking collectives, picked(): lax.all_gather(shard, axis)  32 us
    all_to_all x4, waiting for transfers between devices, copy_for_each(): lax.all_to_all(jnp.broadcast_to(shard[None], (length, *shard.shape)), axi...  25.4 us
    all_to_all x1, blocking collectives, summed_on_arrival(): parts = lax.all_to_all(split_up(shard, dim, length), axis, 0, 0, tiled=True)  18.1 us
    another operation x29, local copies, waits for them, and re-layouts, local(): jax.scipy.linalg.solve_triangular(diag_block, current[offset:offset + PAN...  17.3 us
    unnamed x14, local copies, waits for them, and re-layouts  16.1 us
  transfers between devices with their start and end apart: 5, of which 2 were waited for; matrix products, arithmetic and copies ran while one was open for 25% of the time, Pallas kernels for 0%

commit v1 on v0

v1 whole, which is shorter than its diff:
```python
import jax
import jax.numpy as jnp
from jax import lax
from jax.experimental import pallas as pl
from jax.experimental.pallas import tpu as pltpu
from jax.sharding import PartitionSpec as P

PANEL = 256
GTILES = 16
RB = 128
NZ = 8
HALF = 512
WINDOW = 1024
MESH = pl.DeviceIdType.MESH
BF16 = jnp.bfloat16
F32 = jnp.float32
VMEM = pltpu.VMEM


def dot(a, b):
    return jnp.dot(a, b, preferred_element_type=F32)


def split(value):
    high = value.astype(BF16)
    return high, (value - high.astype(F32)).astype(BF16)


def prepare_kernel(f_ref, m_ref, fm_ref):
    row = lax.axis_index("row")
    col = lax.axis_index("col")
    slot = lax.rem(col, 8)
    d = f_ref[:, pl.ds(pl.multiple_of(slot * RB, RB), RB)].astype(F32)
    r = lax.broadcasted_iota(jnp.int32, (RB, RB), 0)
    c = lax.broadcasted_iota(jnp.int32, (RB, RB), 1)
    inv = jnp.where(r == c, 1.0 / jnp.where(r == c, d, 1.0), 0.0)
    for level in range(7):
        rb = lax.shift_right_logical(r, level)
        cb = lax.shift_right_logical(c, level)
        here = (cb == rb - 1) & ((rb & 1) == 1)
        off = jnp.where(here, d, 0.0).astype(BF16)
        hi, lo = split(inv)
        th, tl = split(dot(off, hi) + dot(off, lo))
        inv = inv - (dot(hi, th) + dot(hi, tl) + dot(lo, th))
    hi, lo = split(inv)
    for j in range(8):
        fj = f_ref[:, j * RB : (j + 1) * RB]
        scaled = dot(hi, fj) + dot(lo, fj)
        m_ref[j] = jnp.where(slot > j, -scaled, jnp.where(slot == j, inv, 0.0)).astype(BF16)
    window = (row == 0) & (col < 8)
    wr = lax.broadcasted_iota(jnp.int32, (RB, WINDOW), 0)
    wc = lax.broadcasted_iota(jnp.int32, (RB, WINDOW), 1)
    pick = jnp.where(wc == wr + slot * RB, 1.0, 0.0)
    fm_ref[...] = jnp.where(window, pick, f_ref[...].astype(F32)).astype(BF16)


def spread_kernel(b_ref, m_ref, ball, mall, own_sem, ra, rb, rm, ssem):
    sub = lax.axis_index("sub")
    row = lax.axis_index("row")
    col = lax.axis_index("col")
    xh, core = row // 2, row % 2
    z, xl = col // 2, col % 2

    def dev(xh_, core_, z_, xl_):
        return (sub, 2 * xh_ + core_, 2 * z_ + xl_)

    sibling = dev(xh, 1 - core, z, xl)
    right = dev(xh, core, (z + 1) % NZ, xl)
    left = dev(xh, core, (z + NZ - 1) % NZ, xl)
    beside = dev(xh, core, z, 1 - xl)
    across = dev(1 - xh, core, z, 1 - xl)
    diagonal = dev(1 - xh, 1 - core, z, 1 - xl)

    barrier = pltpu.get_barrier_semaphore()
    for peer in (sibling, right, left, beside, across, diagonal):
        pl.semaphore_signal(barrier, inc=1, device_id=peer, device_id_type=MESH)
    pl.semaphore_wait(barrier, 6)

    pending = []
    used = [0]

    def copy_of(src, dst, recv, peer, slot):
        return pltpu.make_async_remote_copy(
            src_ref=src, dst_ref=dst, send_sem=ssem.at[slot], recv_sem=recv,
            device_id=peer, device_id_type=MESH,
        )

    def send(src, dst, recv, peer, when=None):
        slot = used[0]
        used[0] += 1

        def start():
            copy_of(src, dst, recv, peer, slot).start()

        def finish():
            copy_of(src, dst, recv, peer, slot).wait_send()

        if when is None:
            start()
        else:
            pl.when(when)(start)
        pending.append((when, finish))

    def finish_all():
        for when, finish in pending:
            if when is None:
                finish()
            else:
                pl.when(when)(finish)
        pending.clear()

    def a_unit(zo, u):
        c = 2 * zo + u
        return ball.at[c, pl.ds(0, HALF)], ra.at[c]

    def b_unit(zo, u):
        c = 2 * zo + u
        return ball.at[c, pl.ds(HALF, HALF)], rb.at[c]

    def m_unit(zo, u, h):
        c = 2 * zo + u
        return mall.at[c, pl.ds(4 * h, 4)], rm.at[h, c]

    def arrive(unit):
        copy_of(unit[0], unit[0], unit[1], sibling, 0).wait_recv()

    def relay(unit, peer, when=None):
        send(unit[0], unit[0], unit[1], peer, when)

    def m_there(zo, h):
        return (zo < 4) if h == 0 else ((zo < 4) & (zo >= 2))

    def handed_out():
        dst, sem = a_unit(z, xl)
        src = b_ref.at[pl.ds(0, HALF)]
        yield None, copy_of(src, dst, sem, beside, 120)
        yield None, copy_of(src, dst, sem, across, 121)
        for h in range(2):
            mdst, msem = m_unit(z, xl, h)
            there = m_there(z, h)
            yield there, copy_of(m_ref.at[pl.ds(4 * h, 4)], mdst, msem, diagonal, 122 + h)
        bdst, bsem = b_unit(z, xl)
        yield None, copy_of(b_ref.at[pl.ds(HALF, HALF)], bdst, bsem, sibling, 124)

    @pl.when(row == 0)
    def _():
        own = pltpu.make_async_copy(b_ref.at[pl.ds(0, HALF)], a_unit(z, xl)[0], own_sem)
        own.start()
        for when, copy in handed_out():
            if when is None:
                copy.start()
            else:
                pl.when(when)(copy.start)
        own.wait()

    @pl.when(core == 0)
    def _():
        def ring_out(zo_right, zo_left, k, u):
            if zo_right is not None and k < (4 if u == 0 else 3):
                relay(a_unit(zo_right, u), right)
            if zo_left is not None and k < (3 if u == 0 else 4):
                relay(a_unit(zo_left, u), left)

        u1 = (xl + xh) % 2
        u2 = 1 - u1

        @pl.when(row != 0)
        def _():
            arrive(a_unit(z, u1))

        relay(a_unit(z, u1), beside, xh == 1)
        relay(a_unit(z, u1), right)
        relay(a_unit(z, u1), left)
        relay(a_unit(z, u1), sibling)
        arrive(a_unit(z, u2))
        relay(a_unit(z, u2), right)
        relay(a_unit(z, u2), left)
        relay(a_unit(z, u2), sibling)
        for k in range(1, 5):
            zl, zr = (z + NZ - k) % NZ, (z + k) % NZ
            for u in range(2):
                if k <= (4 if u == 0 else 3):
                    arrive(a_unit(zl, u))
                    ring_out(zl, None, k, u)
                    relay(a_unit(zl, u), sibling)
                if k <= (3 if u == 0 else 4):
                    arrive(a_unit(zr, u))
                    ring_out(None, zr, k, u)
                    relay(a_unit(zr, u), sibling)
        for c in range(16):
            arrive(b_unit(c // 2, c % 2))
        for c in range(8):
            arrive(m_unit(c // 2, c % 2, 0))
            if c >= 4:
                arrive(m_unit(c // 2, c % 2, 1))
        finish_all()

    def second_chain(own_kind, own_u, other_kind):
        def units(kind, zo, u):
            if kind == "b":
                return [(b_unit(zo, u), None)]
            return [(m_unit(zo, u, h), m_there(zo, h)) for h in range(2)]

        def arrive_if(unit, there):
            if there is None:
                arrive(unit)
            else:
                pl.when(there)(lambda: arrive(unit))

        def ring_step(zo, to_right, to_left):
            for unit, there in units(own_kind, zo, own_u):
                arrive_if(unit, there)
                if to_right:
                    relay(unit, right, there)
                if to_left:
                    relay(unit, left, there)
                relay(unit, across, there)
                relay(unit, beside, there)
                relay(unit, sibling, there)

        def pass_from_beside(kind, zo, u):
            for unit, there in units(kind, zo, u):
                arrive_if(unit, there)
                relay(unit, sibling, there)

        def pass_from_across(kind, zo, u):
            for unit, there in units(kind, zo, u):
                arrive_if(unit, there)
                relay(unit, beside, there)
                relay(unit, sibling, there)

        def others(zo):
            pass_from_across(other_kind, zo, own_u)
            pass_from_beside(own_kind, zo, 1 - own_u)

        def later(zo):
            pass_from_beside(other_kind, zo, 1 - own_u)

        ring_step(z, True, True)
        for k in range(1, 6):
            zl, zr = (z + NZ - k) % NZ, (z + k) % NZ
            if k <= 4:
                ring_step(zl, k < 4, False)
            if k <= 3:
                ring_step(zr, False, k < 3)
            pl_, pr = (z + NZ - (k - 1)) % NZ, (z + (k - 1)) % NZ
            others(pl_)
            if 1 <= k - 1 <= 3:
                others(pr)
            if k >= 2:
                ql, qr = (z + NZ - (k - 2)) % NZ, (z + (k - 2)) % NZ
                later(ql)
                if 1 <= k - 2 <= 3:
                    later(qr)
        later((z + 4) % NZ)
        for c in range(16):
            arrive(a_unit(c // 2, c % 2))
        finish_all()

    @pl.when((core == 1) & (xh == 0))
    def _():
        used[0] = 0
        second_chain("b", xl, "m")

    @pl.when((core == 1) & (xh == 1))
    def _():
        used[0] = 0
        second_chain("m", 1 - xl, "b")

    @pl.when(row == 0)
    def _():
        for when, copy in handed_out():
            if when is None:
                copy.wait_send()
            else:
                pl.when(when)(copy.wait_send)


def solve_kernel(fb_ref, inv_ref, has_ref, b_ref, m_ref, fm_ref, v_ref, s_ref, x_ref):
    row = lax.axis_index("row")
    col = lax.axis_index("col")
    panel = lax.broadcasted_iota(jnp.int32, (WINDOW, 2 * RB), 0) // PANEL
    for b in range(8):
        both = jnp.concatenate([b_ref[2 * b], b_ref[2 * b + 1]], axis=1)
        x_ref[b] = jnp.where(panel >= fb_ref[b], both.astype(F32), 0.0).astype(BF16)
    for i in range(8):
        depth = (i + 1) * RB
        m_rows = jnp.concatenate([m_ref[i, j] for j in range(i + 1)], axis=1)
        for b in range(8):
            x_ref[b, i * RB : depth] = dot(m_rows, x_ref[b, :depth]).astype(BF16)
    fm = fm_ref[...]
    for b in range(8):
        v = dot(fm, x_ref[b]).astype(BF16)
        v_ref[2 * b] = v[:, :RB]
        v_ref[2 * b + 1] = v[:, RB:]
    mine = x_ref[inv_ref[col]].astype(F32).T.astype(BF16)
    half = pl.multiple_of((row % 2) * RB, RB)
    for slot in range(8):
        tile = 2 * slot + row // 2
        live = (has_ref[tile] > 0) & (has_ref[col] > 0)

        @pl.when(live)
        def _():
            other = x_ref[inv_ref[tile], :, pl.ds(half, RB)]
            s_ref[slot] = dot(mine, other).astype(BF16)

        @pl.when(jnp.logical_not(live))
        def _():
            s_ref[slot] = jnp.zeros((2 * RB, RB), BF16)


def exchange_kernel(v_ref, s_ref, vr_ref, sr_ref, vs, vr, ss, sr, own):
    sub = lax.axis_index("sub")
    row = lax.axis_index("row")
    col = lax.axis_index("col")
    cols = lax.axis_size("col")
    subs = lax.axis_size("sub")

    def col_peer(d):
        return (col + d) % cols

    def sub_peer(d):
        return (sub + d) % subs

    barrier = pltpu.get_barrier_semaphore()
    for d in range(1, cols):
        pl.semaphore_signal(barrier, inc=1, device_id=(sub, row, col_peer(d)), device_id_type=MESH)
    for d in range(1, subs):
        pl.semaphore_signal(barrier, inc=1, device_id=(sub_peer(d), row, col), device_id_type=MESH)
    pl.semaphore_wait(barrier, cols + subs - 2)

    copies = []
    for d in (4, 3, 5, 2, 6, 1, 7):
        if d < subs:
            peer = sub_peer(d)
            copies.append(pltpu.make_async_remote_copy(
                src_ref=s_ref.at[peer], dst_ref=sr_ref.at[sub], send_sem=ss.at[d],
                recv_sem=sr.at[d], device_id=(peer, row, col), device_id_type=MESH))
            copies[-1].start()
    for d in (8, 7, 9, 6, 10, 5, 11, 4, 12, 3, 13, 2, 14, 1, 15):
        peer = col_peer(d)
        copies.append(pltpu.make_async_remote_copy(
            src_ref=v_ref.at[peer], dst_ref=vr_ref.at[col], send_sem=vs.at[d],
            recv_sem=vr.at[d], device_id=(sub, row, peer), device_id_type=MESH))
        copies[-1].start()
    mine_v = pltpu.make_async_copy(v_ref.at[col], vr_ref.at[col], own.at[0])
    mine_s = pltpu.make_async_copy(s_ref.at[sub], sr_ref.at[sub], own.at[1])
    mine_v.start()
    mine_s.start()
    mine_v.wait()
    mine_s.wait()
    for copy in copies:
        copy.wait()


def vmem(count):
    return [pl.BlockSpec(memory_space=VMEM)] * count


def local(factor_window, right_sides, first_block, tile_map, interface_block):
    row = lax.axis_index("row")
    factor = factor_window[0]
    sides = right_sides[0]
    shape = jax.ShapeDtypeStruct
    m_own, fm = pl.pallas_call(
        prepare_kernel,
        out_shape=(shape((8, RB, RB), BF16), shape((RB, WINDOW), BF16)),
        in_specs=vmem(1),
        out_specs=tuple(vmem(2)),
    )(factor)
    ball, mall = pl.pallas_call(
        spread_kernel,
        out_shape=(shape((16, WINDOW, RB), BF16), shape((8, 8, RB, RB), BF16)),
        in_specs=vmem(2),
        out_specs=tuple(vmem(2)),
        scratch_shapes=[
            pltpu.SemaphoreType.DMA,
            pltpu.SemaphoreType.DMA((16,)),
            pltpu.SemaphoreType.DMA((16,)),
            pltpu.SemaphoreType.DMA((2, 8)),
            pltpu.SemaphoreType.DMA((128,)),
        ],
        compiler_params=pltpu.CompilerParams(collective_id=0, has_side_effects=True),
    )(sides[:WINDOW], m_own)
    hit = tile_map[0][:, None] == jnp.arange(GTILES, dtype=jnp.int32)[None, :]
    has = jnp.sum(hit.astype(jnp.int32), axis=0)
    where = jnp.sum(jnp.where(hit, jnp.arange(8, dtype=jnp.int32)[:, None], 0), axis=0)
    smem = pl.BlockSpec(memory_space=pltpu.SMEM)
    v_out, s_out = pl.pallas_call(
        solve_kernel,
        out_shape=(shape((16, RB, RB), BF16), shape((8, 2 * RB, RB), BF16)),
        in_specs=[smem, smem, smem] + vmem(3),
        out_specs=tuple(vmem(2)),
        scratch_shapes=[VMEM((8, WINDOW, 2 * RB), BF16)],
    )(first_block[0], where, has, ball, mall, fm)
    subs = lax.axis_size("sub")
    v_in, s_in = pl.pallas_call(
        exchange_kernel,
        out_shape=(shape((16, RB, RB), BF16), shape((subs, 2 * RB, RB), BF16)),
        in_specs=vmem(2),
        out_specs=tuple(vmem(2)),
        scratch_shapes=[
            pltpu.SemaphoreType.DMA((16,)),
            pltpu.SemaphoreType.DMA((16,)),
            pltpu.SemaphoreType.DMA((8,)),
            pltpu.SemaphoreType.DMA((8,)),
            pltpu.SemaphoreType.DMA((2,)),
        ],
        compiler_params=pltpu.CompilerParams(collective_id=1, has_side_effects=True),
    )(v_out, s_out)
    update = v_in.reshape(sides.shape).astype(F32)
    in_window = (row == 0) & (jnp.arange(sides.shape[0], dtype=jnp.int32) < WINDOW)
    updated = jnp.where(in_window[:, None], update, sides.astype(F32) - update)
    schur = interface_block - jnp.sum(s_in.astype(F32), axis=0).T
    return updated.astype(BF16)[None], schur


def solution(mesh):
    placed = (
        P("sub", ("row", "col"), None),
        P("sub", "row", "col"),
        P("sub", None),
        P("sub", None),
        P(("sub", "row"), "col"),
    )
    return jax.shard_map(
        local,
        mesh=mesh,
        in_specs=placed,
        out_specs=(P("sub", "row", "col"), P(("sub", "row"), "col")),
        check_vma=False,
    )
```

time: 354 us -> 95.8 us (0.27); the launches traced: 348 us -> 94.2 us
  waiting for transfers between devices: 88.7 us -> 0 us
  Pallas kernels: 0 us -> 86.4 us
  other arithmetic: 85.2 us -> 4.64 us
  blocking collectives: 59.1 us -> 0 us
  local copies, waits for them, and re-layouts: 38.9 us -> 2.52 us
  starting transfers between devices: 33.7 us -> 0 us
  matrix products: 27.5 us -> 0 us
  between operations: 14.6 us -> 0.68 us
    pallas_call x0 -> x4, Pallas kernels: none -> 86.4 us  [the longest x1 44.7 us: local(): pl.pallas_call(spread_kernel, out_shape=(shape((16, WINDOW, RB), BF16), s...]
    another operation x9 -> x0, other arithmetic: 80.3 us -> none  [local(): jax.scipy.linalg.solve_triangular(diag_block, current[offset:offset + PAN...]
    all_gather x1 -> x0, waiting for transfers between devices: 63.3 us -> none  [whole_of(): shard = lax.all_gather(shard, axis, axis=dim, tiled=True)]
    all_gather x5 -> x0, blocking collectives: 41 us -> none  [the longest x4 32 us: picked(): lax.all_gather(shard, axis)]
    all_to_all x4 -> x0, starting transfers between devices: 33.5 us -> none  [copy_for_each(): lax.all_to_all(jnp.broadcast_to(shard[None], (length, *shard.shape)), axi...]
    all_to_all x4 -> x0, waiting for transfers between devices: 25.4 us -> none  [copy_for_each(): lax.all_to_all(jnp.broadcast_to(shard[None], (length, *shard.shape)), axi...]
    dot_general x13 -> x0, matrix products: 21.1 us -> none  [the longest x8 11.3 us: local(): lax.dot_general(left, my_columns, (((0,), (0,)), ((), ())), preferred_ele...]
    all_to_all x1 -> x0, blocking collectives: 18.1 us -> none  [summed_on_arrival(): parts = lax.all_to_all(split_up(shard, dim, length), axis, 0, 0, tiled=True)]
  transfers between devices with their start and end apart: 5 -> 0, of which waited for: 2 -> 0; matrix products, arithmetic and copies ran while one was open for 25% -> 0% of each run, Pallas kernels for 0% -> 0%
where the time goes in v1:
time: 95.8 us; the launch traced here: 94.2 us
  Pallas kernels  86.4 us (90%)
  other arithmetic  4.64 us (5%)
  local copies, waits for them, and re-layouts  2.52 us (3%)
    pallas_call x1, Pallas kernels, local(): pl.pallas_call(spread_kernel, out_shape=(shape((16, WINDOW, RB), BF16), s...  44.7 us
    pallas_call x1, Pallas kernels, local(): pl.pallas_call(exchange_kernel, out_shape=(shape((16, RB, RB), BF16), sha...  29.8 us
    pallas_call x1, Pallas kernels, local(): pl.pallas_call(solve_kernel, out_shape=(shape((16, RB, RB), BF16), shape(...  7.52 us
    pallas_call x1, Pallas kernels, local(): pl.pallas_call(prepare_kernel, out_shape=(shape((8, RB, RB), BF16), shape...  4.37 us
    convert_element_type x1, other arithmetic, local(): return (updated.astype(BF16)[None], schur)  2.17 us

profile of v1, /device:TPU:1, one launch (start us, length us, event | category | flops | bytes accessed | tf_op | source)
XLA Modules:
  0.0 94.2 jit_solution(17682973915528897235)
XLA Ops:
  0.6 4.4 %shard_map.68 = (bf16[8,128,128]{2,1,0:T(8,128)(2,1)}, bf16[128,1024]{1,0:T(8,128)(2,1)}) custom-call(bf16[128,1024]{1,0:T(8,128)(2,1)} %bitcast.12), custom_call_target="tpu_custom_call" | custom-call | tf_op jit(solution)/shard_map/pallas_call | solution.py:365
  5.0 1.7 %slice_bitcast_fusion.b_ref = bf16[1024,128]{1,0:T(8,128)(2,1)} fusion(bf16[1,2048,128]{2,1,0:T(8,128)(2,1)} %param.6), kind=kLoop, calls=%fused_computation.3 | loop fusion | bytes 524288 | tf_op jit(solution)/shard_map/slice | solution.py:384
  6.7 44.7 %shard_map.69 = (bf16[16,1024,128]{2,1,0:T(8,128)(2,1)}, bf16[8,8,128,128]{3,2,1,0:T(8,128)(2,1)}) custom-call(bf16[1024,128]{1,0:T(8,128)(2,1)} %slice_bitcast_fusion.b_ref, bf16[8,128,128]{2,1,0:T(8,128)(2,1)} %get-tuple-element.10.m_ref), custom_call_target="tpu_custom_call" | custom-call | tf_op jit(solution)/shard_map/pallas_call | solution.py:371
  51.4 0.0 copy-start.1
  51.4 1.3 %convert_reduce_fusion.1 = (s32[16]{0:T(128)}, s32[16]{0:T(128)}) fusion(s32[8]{0:T(128)} %bitcast.14), kind=kLoop, calls=%fused_computation.7 | loop fusion | flops 608 | bytes 160 | tf_op jit(solution)/shard_map/reduce_sum | solution.py:386
  52.7 0.0 copy-start
  52.7 7.5 %shard_map.70 = (bf16[16,128,128]{2,1,0:T(8,128)(2,1)}, bf16[8,256,128]{2,1,0:T(8,128)(2,1)}) custom-call(s32[8]{0:T(128)} %bitcast.13, s32[16]{0:T(128)} %get-tuple-element.23.inv_ref, s32[16]{0:T(128)} %get-tuple-element.22.has_ref, bf16[16,1024,128]{2,1,0:T(8,128)(2,1)} %get-tuple-element.11.b_ref, bf16[8,8,128,128]{3,2,1,0:T(8,128)(2,1)} %get-tuple-element.12.m_ref, ...), custom_call_target="tpu_custom_call" | custom-call | tf_op jit(solution)/shard_map/pallas_call | solution.py:389
  60.3 29.8 %shard_map.71 = (bf16[16,128,128]{2,1,0:T(8,128)(2,1)}, bf16[8,256,128]{2,1,0:T(8,128)(2,1)}) custom-call(bf16[16,128,128]{2,1,0:T(8,128)(2,1)} %get-tuple-element.14.v_ref, bf16[8,256,128]{2,1,0:T(8,128)(2,1)} %get-tuple-element.15.s_ref), custom_call_target="tpu_custom_call" | custom-call | tf_op jit(solution)/shard_map/pallas_call | solution.py:397
  90.0 1.1 %convert_reduce_fusion = f32[256,128]{1,0:T(8,128)S(1)} fusion(bf16[8,256,128]{2,1,0:T(8,128)(2,1)} %get-tuple-element.17), kind=kLoop, calls=%fused_computation.2 | loop fusion | flops 491520 | bytes 655360 | tf_op jit(solution)/shard_map/reduce_sum | solution.py:414
  91.2 0.0 copy-done.1
  91.2 0.1 copy.9
  91.3 0.8 copy.10
  92.0 0.0 copy-done
  92.0 2.2 %fusion = bf16[1,2048,128]{2,1,0:T(8,128)(2,1)} fusion(bf16[1,2048,128]{2,1,0:T(8,128)(2,1)S(1)} %copy-done, pred[2048]{0:T(1024)(128)(4,1)S(1)} %fusion.1, bf16[1,2048,128]{2,1,0:T(8,128)(2,1)} %bitcast.11), kind=kLoop, calls=%fused_computation.1 | loop fusion | flops 1310720 | bytes 1574912 | tf_op jit(solution)/shard_map/convert_element_type | solution.py:415
  (2 shorter events, 0.0 us)
Async XLA Ops:
  51.4 39.7 %copy-start.1 = (f32[128,256]{1,0:T(8,128)S(1)}, f32[128,256]{1,0:T(8,128)}, u32[]{:S(2)}) copy-start(f32[128,256]{1,0:T(8,128)} %param.9) | copy-start | bytes 393220
  52.7 39.3 %copy-start = (bf16[1,2048,128]{2,1,0:T(8,128)(2,1)S(1)}, bf16[1,2048,128]{2,1,0:T(8,128)(2,1)}, u32[]{:S(2)}) copy-start(bf16[1,2048,128]{2,1,0:T(8,128)(2,1)} %param.6) | copy-start | bytes 1572868

commit v2 on v0

v2 whole, which is shorter than its diff:
```python
import jax
import jax.numpy as jnp
from jax import lax
from jax.experimental import pallas as pl
from jax.experimental.pallas import tpu as pltpu
from jax.sharding import PartitionSpec as P

PANEL = 256
RB = 128
NZ = 8
WINDOW = 1024
SLOTS = 256
GROUPS = ((4, 3, 5, 2), (6, 1, 7, 0))
SPLIT = 640
A_PARTS = ((0, 320), (320, 320))
B_PARTS = ((640, 192), (832, 192))
MESH = pl.DeviceIdType.MESH
BF16 = jnp.bfloat16
F32 = jnp.float32
VMEM = pltpu.VMEM


def dot(a, b):
    return jnp.dot(a, b, preferred_element_type=F32)


def split(value):
    high = value.astype(BF16)
    return high, (value - high.astype(F32)).astype(BF16)


def inverse_rows(f_ref, m_ref, slot):
    d = f_ref[:, pl.ds(pl.multiple_of(slot * RB, RB), RB)].astype(F32)
    r = lax.broadcasted_iota(jnp.int32, (RB, RB), 0)
    c = lax.broadcasted_iota(jnp.int32, (RB, RB), 1)
    inv = jnp.where(r == c, 1.0 / jnp.where(r == c, d, 1.0), 0.0)
    for level in range(7):
        rb = lax.shift_right_logical(r, level)
        cb = lax.shift_right_logical(c, level)
        here = (cb == rb - 1) & ((rb & 1) == 1)
        off = jnp.where(here, d, 0.0).astype(BF16)
        hi, lo = split(inv)
        th, tl = split(dot(off, hi) + dot(off, lo))
        inv = inv - (dot(hi, th) + dot(hi, tl) + dot(lo, th))
    hi, lo = split(inv)
    for j in range(8):
        fj = f_ref[:, j * RB : (j + 1) * RB]
        scaled = dot(hi, fj) + dot(lo, fj)
        m_ref[j] = jnp.where(slot > j, -scaled, jnp.where(slot == j, inv, 0.0)).astype(BF16)


def whole_kernel(
    fb_ref, tm_ref, sides_ref, factor_ref, vin_ref, sin_ref,
    b_ref, f_ref, m_ref, ball, mall, x_ref, v_ref, s_ref, fm_ref,
    own_sem, ra, rb, rm, ssem, hsem, vs, vr, ss, sr,
):
    sub = lax.axis_index("sub")
    row = lax.axis_index("row")
    col = lax.axis_index("col")
    xh, core = row // 2, row % 2
    z, xl = col // 2, col % 2

    def dev(xh_, core_, z_, xl_):
        return (sub, 2 * xh_ + core_, 2 * z_ + xl_)

    z_up, z_down = (z + 1) % NZ, (z + NZ - 1) % NZ
    sibling = dev(xh, 1 - core, z, xl)
    right = dev(xh, core, z_up, xl)
    left = dev(xh, core, z_down, xl)
    beside = dev(xh, core, z, 1 - xl)
    across = dev(1 - xh, core, z, 1 - xl)
    other_beside = dev(xh, 1 - core, z, 1 - xl)
    other_far = dev(1 - xh, 1 - core, z, xl)
    diagonal = dev(1 - xh, 1 - core, z, 1 - xl)
    right_2 = dev(xh, core, (z + 2) % NZ, xl)
    left_2 = dev(xh, core, (z + NZ - 2) % NZ, xl)
    reach = (2, NZ - 2, 1, NZ - 1)
    other_column = [dev(xh, 1 - core, (z + d) % NZ, xl) for d in reach]
    far = dev(1 - xh, core, z, xl)
    x = 2 * xh + xl

    cols = lax.axis_size("col")
    subs = lax.axis_size("sub")
    b_in = pltpu.make_async_copy(sides_ref.at[0, pl.ds(0, WINDOW)], b_ref, own_sem.at[0])
    f_in = pltpu.make_async_copy(factor_ref.at[0], f_ref, own_sem.at[1])
    b_in.start()
    f_in.start()
    barrier = pltpu.get_barrier_semaphore()
    near = [sibling, across, other_beside, other_far, diagonal, far] + other_column
    for peer in near:
        pl.semaphore_signal(barrier, inc=1, device_id=peer, device_id_type=MESH)
    for d in range(1, cols):
        pl.semaphore_signal(barrier, inc=1, device_id=(sub, row, (col + d) % cols), device_id_type=MESH)
    for d in range(1, subs):
        pl.semaphore_signal(barrier, inc=1, device_id=((sub + d) % subs, row, col), device_id_type=MESH)
    b_in.wait()
    f_in.wait()
    pl.semaphore_wait(barrier, len(near) + cols + subs - 2)

    pending = {}
    used = [0]

    def copy_of(src, dst, recv, peer, slot):
        return pltpu.make_async_remote_copy(
            src_ref=src, dst_ref=dst, send_sem=ssem.at[slot], recv_sem=recv,
            device_id=peer, device_id_type=MESH,
        )

    def send(src, dst, recv, peer, when=None):
        slot = used[0] % SLOTS
        used[0] += 1
        finish_one(slot)

        def start():
            copy_of(src, dst, recv, peer, slot).start()

        def finish():
            copy_of(src, dst, recv, peer, slot).wait_send()

        if when is None:
            start()
        else:
            pl.when(when)(start)
        pending[slot] = (when, finish)

    def finish_one(slot):
        if slot in pending:
            when, finish = pending.pop(slot)
            if when is None:
                finish()
            else:
                pl.when(when)(finish)

    def finish_all():
        for slot in list(pending):
            finish_one(slot)

    def a_units(zo, u):
        c = 2 * zo + u
        return [(ball.at[c, pl.ds(lo, n)], ra.at[p, c]) for p, (lo, n) in enumerate(A_PARTS)]

    def b_units(zo, u):
        c = 2 * zo + u
        return [(ball.at[c, pl.ds(lo, n)], rb.at[p, c]) for p, (lo, n) in enumerate(B_PARTS)]

    def m_unit(zo, u, h):
        c = 2 * zo + u
        return mall.at[c, pl.ds(2 * h, 2)], rm.at[h, c]

    def arrive(unit):
        copy_of(unit[0], unit[0], unit[1], sibling, 0).wait_recv()

    def relay(unit, peer, when=None):
        send(unit[0], unit[0], unit[1], peer, when)

    def m_there(zo, h):
        return (zo < 4) & (zo >= h)

    def hand(src, dst, sem, peer, slot):
        return pltpu.make_async_remote_copy(
            src_ref=src, dst_ref=dst, send_sem=hsem.at[slot], recv_sem=sem,
            device_id=peer, device_id_type=MESH,
        )

    def sides_out():
        slot = 0
        for p, (lo, n) in enumerate(A_PARTS):
            dst, sem = a_units(z, xl)[p]
            for peer in (other_far, diagonal, other_beside, sibling):
                yield hand(b_ref.at[pl.ds(lo, n)], dst, sem, peer, slot)
                slot += 1
        for p, (lo, n) in enumerate(B_PARTS):
            dst, sem = b_units(z, xl)[p]
            for peer in other_column + [sibling]:
                yield hand(b_ref.at[pl.ds(lo, n)], dst, sem, peer, slot)
                slot += 1

    def factors_out():
        for h in range(4):
            dst, sem = m_unit(z, xl, h)
            src = m_ref.at[pl.ds(2 * h, 2)]
            there = m_there(z, h)
            yield there & (xl != h), hand(src, dst, sem, dev(h // 2, core, z, h % 2), 4 * len(A_PARTS) + 5 * len(B_PARTS) + h)

    def factors_kept():
        for h in range(2):
            dst, sem = m_unit(z, xl, h)
            src = m_ref.at[pl.ds(2 * h, 2)]
            yield m_there(z, h) & (xl == h), pltpu.make_async_copy(src, dst, sem)

    @pl.when(row == 0)
    def _():
        for copy in sides_out():
            copy.start()

        @pl.when(col < 8)
        def _():
            inverse_rows(f_ref, m_ref, lax.rem(col, 8))
            for when, copy in factors_out():
                pl.when(when)(copy.start)
            for when, copy in factors_kept():
                pl.when(when)(copy.start)

    slot8 = lax.rem(col, 8)
    wr = lax.broadcasted_iota(jnp.int32, (RB, WINDOW), 0)
    wc = lax.broadcasted_iota(jnp.int32, (RB, WINDOW), 1)
    pick = jnp.where(wc == wr + slot8 * RB, 1.0, 0.0)
    fm_ref[...] = jnp.where((row == 0) & (col < 8), pick, f_ref[...].astype(F32)).astype(BF16)

    def spots(d):
        return {0: (z,), 4: ((z + 4) % NZ,)}.get(d, ((z + NZ - d) % NZ, (z + d) % NZ))

    def pass_b(zo, u, peers):
        for unit in b_units(zo, u):
            arrive(unit)
            for peer in peers:
                relay(unit, peer)

    def pass_m(zo, h, peers):
        there = m_there(zo, h)
        for u in range(2):
            unit = m_unit(zo, u, h)
            pl.when(there)(lambda: arrive(unit))
            for peer in peers:
                relay(unit, peer, there)

    def onward(d, side):
        if d == 2:
            return (right, right_2) if side == 0 else (left,)
        return ()

    def b_steps(home, own_u):
        steps = []
        for d in range(5):
            at = 1 if d < 3 else 2
            for side, zo in enumerate(spots(d)):
                first = onward(d, side) + (across, beside, sibling) if home else (beside, sibling)
                steps.append((at if home else at + 1, lambda zo=zo, f=first: pass_b(zo, own_u, f)))
                later = lambda zo=zo: pass_b(zo, 1 - own_u, (sibling,))
                steps.append((at + 1 if home else at + 2, later))
        return steps

    def m_steps():
        steps = []
        for d in range(5):
            at = (1, 2, 2, 3, 3)[d]
            for side, zo in enumerate(spots(d)):
                first = (right_2, left_2, right, left) if d == 0 else onward(d, side)
                first = first + (far, across, beside, sibling)
                steps.append((at, lambda zo=zo, f=first: pass_m(zo, x, f)))
                for h in (2 * xh + 1 - xl, 3 - x, 2 * (1 - xh) + xl):
                    steps.append((at + 1, lambda zo=zo, h=h: pass_m(zo, h, (sibling,))))
        return steps

    def a_steps():
        def start():
            for p in range(len(A_PARTS)):
                for u in range(2):
                    unit = a_units(z, u)[p]
                    arrive(unit)
                    for peer in (right, left, sibling):
                        relay(unit, peer)

        def step(k):
            zl, zr = (z + NZ - k) % NZ, (z + k) % NZ
            for p in range(len(A_PARTS)):
                for u in range(2):
                    last_l, last_r = (4, 3) if u == 0 else (3, 4)
                    if k <= last_l:
                        unit = a_units(zl, u)[p]
                        arrive(unit)
                        if k < last_l:
                            relay(unit, right)
                        relay(unit, sibling)
                    if k <= last_r:
                        unit = a_units(zr, u)[p]
                        arrive(unit)
                        if k < last_r:
                            relay(unit, left)
                        relay(unit, sibling)

        return [(1, start)] + [(1 + k, lambda k=k: step(k)) for k in range(1, 5)]

    def walk(steps, rest):
        used[0] = 0
        for _, step in sorted(steps, key=lambda item: item[0]):
            step()
        for unit in rest():
            arrive(unit)
        finish_all()

    def sides_left():
        return [x for c in range(16) for x in a_units(c // 2, c % 2) + b_units(c // 2, c % 2)]

    def factors_left():
        return [m_unit(c // 2, c % 2, h) for c in range(8) for h in range(c // 2 + 1)]

    @pl.when(core == 0)
    def _():
        walk(m_steps(), sides_left)

    @pl.when((core == 1) & (xh == 0))
    def _():
        walk(a_steps() + b_steps(True, xl), factors_left)

    @pl.when((core == 1) & (xh == 1))
    def _():
        walk(a_steps() + b_steps(False, 1 - xl), factors_left)

    @pl.when(row == 0)
    def _():
        for copy in sides_out():
            copy.wait_send()
        for when, copy in factors_out():
            pl.when(when)(copy.wait_send)

    panel = lax.broadcasted_iota(jnp.int32, (WINDOW, 2 * RB), 0) // PANEL

    def solve(group):
        for o in group:
            b = (z + o) % NZ
            both = jnp.concatenate([ball[2 * b], ball[2 * b + 1]], axis=1)
            x_ref[o] = jnp.where(panel >= fb_ref[0, b], both.astype(F32), 0.0).astype(BF16)
        for i in range(8):
            depth = (i + 1) * RB
            m_rows = jnp.concatenate([mall[i, j] for j in range(i + 1)], axis=1)
            for o in group:
                x_ref[o, i * RB : depth] = dot(m_rows, x_ref[o, :depth]).astype(BF16)

    fm = fm_ref[...]

    def update(o):
        v = dot(fm, x_ref[o]).astype(BF16)
        v_ref[2 * o] = v[:, :RB]
        v_ref[2 * o + 1] = v[:, RB:]

    def v_copy(o, u):
        return pltpu.make_async_remote_copy(
            src_ref=v_ref.at[2 * o + u], dst_ref=vin_ref.at[col], send_sem=vs.at[2 * o + u],
            recv_sem=vr.at[col], device_id=(sub, row, 2 * ((z + o) % NZ) + u), device_id_type=MESH)

    def v_each(o, act):
        for u in range(2):
            if o == 0:
                pl.when(u != xl)(lambda: act(v_copy(0, u)))
            else:
                act(v_copy(o, u))

    def v_send(o):
        v_each(o, lambda copy: copy.start())

    def tile_of(g):
        where, hits = jnp.int32(0), jnp.int32(0)
        for b in range(8):
            hit = tm_ref[0, b] == g
            where = jnp.where(hit, b, where)
            hits = jnp.where(hit, 1, hits)
        return where, hits

    def s_copy(d):
        peer = (sub + d) % subs
        return pltpu.make_async_remote_copy(
            src_ref=s_ref.at[d], dst_ref=sin_ref.at[sub], send_sem=ss.at[d],
            recv_sem=sr.at[sub], device_id=(peer, row, col), device_id_type=MESH)

    groups = GROUPS
    solve(groups[0])
    for n, o in enumerate(groups[0]):
        update(o)
        if n:
            v_send(groups[0][n - 1])
    solve(groups[1])
    v_send(groups[0][-1])

    where, mine_hits = tile_of(col)
    mine = x_ref[(where + NZ - z) % NZ].astype(F32).T.astype(BF16)
    half = pl.multiple_of(core * RB, RB)
    far_first = [d for d in (4, 3, 5, 2, 6, 1, 7, 0) if d < subs]
    for n, d in enumerate(far_first):
        slot = (sub + d) % subs
        place, hits = tile_of(2 * slot + xh)
        part = dot(mine, x_ref[(place + NZ - z) % NZ, :, pl.ds(half, RB)])
        s_ref[d] = jnp.where(hits * mine_hits > 0, part, 0.0).astype(BF16)
        if n:
            s_copy(far_first[n - 1]).start()
    mine_s = pltpu.make_async_copy(s_ref.at[0], sin_ref.at[sub], own_sem.at[0])
    for n, o in enumerate(groups[1]):
        update(o)
        if n:
            v_send(groups[1][n - 1])
        else:
            mine_s.start()
    mine_v = pltpu.make_async_copy(v_ref.at[xl], vin_ref.at[col], own_sem.at[1])
    mine_s.wait()
    v_send(0)
    mine_v.start()
    mine_v.wait()

    for d in range(1, subs):
        s_copy(d).wait_send()
        source = (sub + d) % subs
        pltpu.make_async_remote_copy(
            src_ref=s_ref.at[d], dst_ref=sin_ref.at[source], send_sem=ss.at[d],
            recv_sem=sr.at[source], device_id=(source, row, col), device_id_type=MESH).wait_recv()
    for o in range(8):
        v_each(o, lambda copy: copy.wait_send())
    for d in range(1, cols):
        source = (col + d) % cols
        pltpu.make_async_remote_copy(
            src_ref=v_ref.at[0], dst_ref=vin_ref.at[source], send_sem=vs.at[0],
            recv_sem=vr.at[source], device_id=(sub, row, source), device_id_type=MESH).wait_recv()


def local(factor_window, right_sides, first_block, tile_map, interface_block):
    row = lax.axis_index("row")
    sides = right_sides[0]
    subs = lax.axis_size("sub")
    shape = jax.ShapeDtypeStruct
    vmem = pl.BlockSpec(memory_space=VMEM)
    smem = pl.BlockSpec(memory_space=pltpu.SMEM)
    anywhere = pl.BlockSpec(memory_space=pl.ANY)
    dma = pltpu.SemaphoreType.DMA
    v_in, s_in = pl.pallas_call(
        whole_kernel,
        out_shape=(shape((16, RB, RB), BF16), shape((subs, 2 * RB, RB), BF16)),
        in_specs=[smem, smem, anywhere, anywhere],
        out_specs=(vmem, vmem),
        scratch_shapes=[
            VMEM((WINDOW, RB), BF16),
            VMEM((RB, WINDOW), BF16),
            VMEM((8, RB, RB), BF16),
            VMEM((16, WINDOW, RB), BF16),
            VMEM((8, 8, RB, RB), BF16),
            VMEM((8, WINDOW, 2 * RB), BF16),
            VMEM((16, RB, RB), BF16),
            VMEM((8, 2 * RB, RB), BF16),
            VMEM((RB, WINDOW), BF16),
            dma((2,)),
            dma((len(A_PARTS), 16)),
            dma((len(B_PARTS), 16)),
            dma((4, 8)),
            dma((SLOTS,)),
            dma((48,)),
            dma((16,)),
            dma((16,)),
            dma((8,)),
            dma((8,)),
        ],
        compiler_params=pltpu.CompilerParams(collective_id=0, has_side_effects=True),
    )(first_block, tile_map, right_sides, factor_window)
    update = v_in.reshape(sides.shape).astype(F32)
    in_window = (row == 0) & (jnp.arange(sides.shape[0], dtype=jnp.int32) < WINDOW)
    updated = jnp.where(in_window[:, None], update, sides.astype(F32) - update)
    schur = interface_block - jnp.sum(s_in.astype(F32), axis=0).T
    return updated.astype(BF16)[None], schur


def solution(mesh):
    placed = (
        P("sub", ("row", "col"), None),
        P("sub", "row", "col"),
        P("sub", None),
        P("sub", None),
        P(("sub", "row"), "col"),
    )
    return jax.shard_map(
        local,
        mesh=mesh,
        in_specs=placed,
        out_specs=(P("sub", "row", "col"), P(("sub", "row"), "col")),
        check_vma=False,
    )
```

time: 354 us -> 75.3 us (0.21); the launches traced: 348 us -> 75.2 us
  waiting for transfers between devices: 88.7 us -> 0 us
  other arithmetic: 85.2 us -> 2.33 us
  Pallas kernels: 0 us -> 70.5 us
  blocking collectives: 59.1 us -> 0 us
  local copies, waits for them, and re-layouts: 38.9 us -> 1.68 us
  starting transfers between devices: 33.7 us -> 0 us
  matrix products: 27.5 us -> 0 us
  between operations: 14.6 us -> 0.69 us
    another operation x9 -> x0, other arithmetic: 80.3 us -> none  [local(): jax.scipy.linalg.solve_triangular(diag_block, current[offset:offset + PAN...]
    pallas_call x0 -> x1, Pallas kernels: none -> 70.5 us  [local(): pl.pallas_call(whole_kernel, out_shape=(shape((16, RB, RB), BF16), shape(...]
    all_gather x1 -> x0, waiting for transfers between devices: 63.3 us -> none  [whole_of(): shard = lax.all_gather(shard, axis, axis=dim, tiled=True)]
    all_gather x5 -> x0, blocking collectives: 41 us -> none  [the longest x4 32 us: picked(): lax.all_gather(shard, axis)]
    all_to_all x4 -> x0, starting transfers between devices: 33.5 us -> none  [copy_for_each(): lax.all_to_all(jnp.broadcast_to(shard[None], (length, *shard.shape)), axi...]
    all_to_all x4 -> x0, waiting for transfers between devices: 25.4 us -> none  [copy_for_each(): lax.all_to_all(jnp.broadcast_to(shard[None], (length, *shard.shape)), axi...]
    dot_general x13 -> x0, matrix products: 21.1 us -> none  [the longest x8 11.3 us: local(): lax.dot_general(left, my_columns, (((0,), (0,)), ((), ())), preferred_ele...]
    all_to_all x1 -> x0, blocking collectives: 18.1 us -> none  [summed_on_arrival(): parts = lax.all_to_all(split_up(shard, dim, length), axis, 0, 0, tiled=True)]
  transfers between devices with their start and end apart: 5 -> 0, of which waited for: 2 -> 0; matrix products, arithmetic and copies ran while one was open for 25% -> 0% of each run, Pallas kernels for 0% -> 0%
where the time goes in v2:
time: 75.3 us; the launch traced here: 75.2 us
  Pallas kernels  70.5 us (94%)
  other arithmetic  2.33 us (3%)
  local copies, waits for them, and re-layouts  1.68 us (2%)
    pallas_call x1, Pallas kernels, local(): pl.pallas_call(whole_kernel, out_shape=(shape((16, RB, RB), BF16), shape(...  70.5 us
    convert_element_type x1, other arithmetic, local(): return (updated.astype(BF16)[None], schur)  2.23 us
    unnamed x8, local copies, waits for them, and re-layouts  1.68 us

profile of v2, /device:TPU:1, one launch (start us, length us, event | category | flops | bytes accessed | tf_op | source)
XLA Modules:
  0.0 75.2 jit_solution(14521400795401695531)
XLA Ops:
  0.6 0.0 copy-start
  0.6 70.5 %shard_map.68 = (bf16[16,128,128]{2,1,0:T(8,128)(2,1)}, bf16[8,256,128]{2,1,0:T(8,128)(2,1)}) custom-call(s32[1,8]{1,0:T(1,128)} %fb_ref.1, s32[1,8]{1,0:T(1,128)} %tm_ref.1, bf16[1,2048,128]{2,1,0:T(8,128)(2,1)} %sides_ref.1, bf16[1,128,1024]{2,1,0:T(8,128)(2,1)} %factor_ref.1), custom_call_target="tpu_custom_call" | custom-call | tf_op jit(solution)/shard_map/pallas_call | solution.py:423
  71.1 0.0 copy-done
  71.1 0.0 copy-start.1
  71.1 2.2 %fusion = bf16[1,2048,128]{2,1,0:T(8,128)(2,1)} fusion(bf16[1,2048,128]{2,1,0:T(8,128)(2,1)S(1)} %copy-done, pred[2048]{0:T(1024)(128)(4,1)S(1)} %fusion.1, bf16[1,2048,128]{2,1,0:T(8,128)(2,1)} %bitcast.6), kind=kLoop, calls=%fused_computation.1 | loop fusion | flops 1310720 | bytes 1574912 | tf_op jit(solution)/shard_map/convert_element_type | solution.py:455
  73.4 0.0 copy-done.1
  73.4 0.0 copy-start.2
  73.4 0.1 convert_reduce_fusion
  73.5 0.8 %copy-done.2 = f32[128,256]{1,0:T(8,128)S(1)} copy-done((f32[128,256]{1,0:T(8,128)S(1)}, f32[128,256]{1,0:T(8,128)}, u32[]{:S(2)}) %copy-start.2) | copy-done | bytes 131096
  74.3 0.1 copy.7
  74.4 0.8 %copy.8 = f32[128,256]{1,0:T(8,128)} copy(f32[128,256]{0,1:T(8,128)S(1)} %bitcast_subtract_fusion) | data formatting | bytes 262144
  (2 shorter events, 0.0 us)
Async XLA Ops:
  0.6 70.5 %copy-start = (bf16[1,2048,128]{2,1,0:T(8,128)(2,1)S(1)}, bf16[1,2048,128]{2,1,0:T(8,128)(2,1)}, u32[]{:S(2)}) copy-start(bf16[1,2048,128]{2,1,0:T(8,128)(2,1)} %sides_ref.1) | copy-start | bytes 1572868
  71.1 2.2 %copy-start.1 = (bf16[8,256,128]{2,1,0:T(8,128)(2,1)S(1)}, bf16[8,256,128]{2,1,0:T(8,128)(2,1)}, u32[]{:S(2)}) copy-start(bf16[8,256,128]{2,1,0:T(8,128)(2,1)} %get-tuple-element.5) | copy-start | bytes 1572868
  73.4 0.9 %copy-start.2 = (f32[128,256]{1,0:T(8,128)S(1)}, f32[128,256]{1,0:T(8,128)}, u32[]{:S(2)}) copy-start(f32[128,256]{1,0:T(8,128)} %param.9) | copy-start | bytes 393220

commit v3 on v2

--- a/solution.py
+++ b/solution.py
@@ -50,8 +50,8 @@
 
 
 def whole_kernel(
-    fb_ref, tm_ref, sides_ref, factor_ref, vin_ref, sin_ref,
-    b_ref, f_ref, m_ref, ball, mall, x_ref, v_ref, s_ref, fm_ref,
+    fb_ref, tm_ref, sides_ref, factor_ref, block_ref, updated_ref, schur_ref,
+    vin_ref, sin_ref, b_ref, f_ref, m_ref, ball, mall, x_ref, v_ref, s_ref, fm_ref,
     own_sem, ra, rb, rm, ssem, hsem, vs, vr, ss, sr,
 ):
     sub = lax.axis_index("sub")
@@ -81,7 +81,13 @@
 
     cols = lax.axis_size("col")
     subs = lax.axis_size("sub")
-    b_in = pltpu.make_async_copy(sides_ref.at[0, pl.ds(0, WINDOW)], b_ref, own_sem.at[0])
+    below = b_ref.shape[0] - WINDOW
+    b_in = pltpu.make_async_copy(
+        sides_ref.at[0, pl.ds(0, WINDOW)], b_ref.at[pl.ds(0, WINDOW)], own_sem.at[0]
+    )
+    rest_in = pltpu.make_async_copy(
+        sides_ref.at[0, pl.ds(WINDOW, below)], b_ref.at[pl.ds(WINDOW, below)], own_sem.at[2]
+    )
     f_in = pltpu.make_async_copy(factor_ref.at[0], f_ref, own_sem.at[1])
     b_in.start()
     f_in.start()
@@ -95,6 +101,7 @@
         pl.semaphore_signal(barrier, inc=1, device_id=((sub + d) % subs, row, col), device_id_type=MESH)
     b_in.wait()
     f_in.wait()
+    rest_in.start()
     pl.semaphore_wait(barrier, len(near) + cols + subs - 2)
 
     pending = {}
@@ -396,23 +403,37 @@
     mine_v.start()
     mine_v.wait()
 
+    rest_in.wait()
+    total = sin_ref[sub].astype(F32)
     for d in range(1, subs):
-        s_copy(d).wait_send()
         source = (sub + d) % subs
         pltpu.make_async_remote_copy(
             src_ref=s_ref.at[d], dst_ref=sin_ref.at[source], send_sem=ss.at[d],
             recv_sem=sr.at[source], device_id=(source, row, col), device_id_type=MESH).wait_recv()
-    for o in range(8):
-        v_each(o, lambda copy: copy.wait_send())
-    for d in range(1, cols):
+        total = total + sin_ref[source].astype(F32)
+    schur_ref[:, :RB] = block_ref[:, :RB] - total[:RB].T
+    schur_ref[:, RB:] = block_ref[:, RB:] - total[RB:].T
+
+    def finish_rows(source):
+        rows = pl.ds(pl.multiple_of(source * RB, RB), RB)
+        v = vin_ref[source].astype(F32)
+        solved = (row == 0) & (source < 8)
+        updated_ref[rows] = jnp.where(solved, v, b_ref[rows].astype(F32) - v).astype(BF16)
+
+    finish_rows(col)
+    for d in (2, 14, 1, 15, 3, 13, 4, 12, 5, 11, 6, 10, 7, 9, 8):
         source = (col + d) % cols
         pltpu.make_async_remote_copy(
             src_ref=v_ref.at[0], dst_ref=vin_ref.at[source], send_sem=vs.at[0],
             recv_sem=vr.at[source], device_id=(sub, row, source), device_id_type=MESH).wait_recv()
+        finish_rows(source)
+    for d in range(1, subs):
+        s_copy(d).wait_send()
+    for o in range(8):
+        v_each(o, lambda copy: copy.wait_send())
 
 
 def local(factor_window, right_sides, first_block, tile_map, interface_block):
-    row = lax.axis_index("row")
     sides = right_sides[0]
     subs = lax.axis_size("sub")
     shape = jax.ShapeDtypeStruct
@@ -420,13 +441,15 @@
     smem = pl.BlockSpec(memory_space=pltpu.SMEM)
     anywhere = pl.BlockSpec(memory_space=pl.ANY)
     dma = pltpu.SemaphoreType.DMA
-    v_in, s_in = pl.pallas_call(
+    updated, schur = pl.pallas_call(
         whole_kernel,
-        out_shape=(shape((16, RB, RB), BF16), shape((subs, 2 * RB, RB), BF16)),
-        in_specs=[smem, smem, anywhere, anywhere],
+        out_shape=(shape(sides.shape, BF16), shape(interface_block.shape, F32)),
+        in_specs=[smem, smem, anywhere, anywhere, vmem],
         out_specs=(vmem, vmem),
         scratch_shapes=[
-            VMEM((WINDOW, RB), BF16),
+            VMEM((16, RB, RB), BF16),
+            VMEM((subs, 2 * RB, RB), BF16),
+            VMEM(sides.shape, BF16),
             VMEM((RB, WINDOW), BF16),
             VMEM((8, RB, RB), BF16),
             VMEM((16, WINDOW, RB), BF16),
@@ -435,7 +458,7 @@
             VMEM((16, RB, RB), BF16),
             VMEM((8, 2 * RB, RB), BF16),
             VMEM((RB, WINDOW), BF16),
-            dma((2,)),
+            dma((3,)),
             dma((len(A_PARTS), 16)),
             dma((len(B_PARTS), 16)),
             dma((4, 8)),
@@ -447,12 +470,8 @@
             dma((8,)),
         ],
         compiler_params=pltpu.CompilerParams(collective_id=0, has_side_effects=True),
-    )(first_block, tile_map, right_sides, factor_window)
-    update = v_in.reshape(sides.shape).astype(F32)
-    in_window = (row == 0) & (jnp.arange(sides.shape[0], dtype=jnp.int32) < WINDOW)
-    updated = jnp.where(in_window[:, None], update, sides.astype(F32) - update)
-    schur = interface_block - jnp.sum(s_in.astype(F32), axis=0).T
-    return updated.astype(BF16)[None], schur
+    )(first_block, tile_map, right_sides, factor_window, interface_block)
+    return updated[None], schur
 
 
 def solution(mesh):

time: 75.3 us -> 74.1 us (0.984)
  other arithmetic: 2.33 us -> 0 us
  local copies, waits for them, and re-layouts: 1.68 us -> 2.56 us
    convert_element_type x1 -> x0, other arithmetic: 2.23 us -> none  [local(): return (updated.astype(BF16)[None], schur)]
    unnamed x8 -> x4, local copies, waits for them, and re-layouts: 1.68 us -> 2.56 us
where the time goes in v3:
time: 74.1 us; the launch traced here: 74 us
  Pallas kernels  70.8 us (96%)
  local copies, waits for them, and re-layouts  2.56 us (3%)
    pallas_call x1, Pallas kernels, local(): pl.pallas_call(whole_kernel, out_shape=(shape(sides.shape, BF16), shape(i...  70.8 us
    unnamed x4, local copies, waits for them, and re-layouts  2.56 us

profile of v3, /device:TPU:1, one launch (start us, length us, event | category | flops | bytes accessed | tf_op | source)
XLA Modules:
  0.0 74.0 jit_solution(2897969374710813274)
XLA Ops:
  0.6 70.8 %shard_map.68 = (bf16[2048,128]{1,0:T(8,128)(2,1)}, f32[128,256]{1,0:T(8,128)}) custom-call(s32[1,8]{1,0:T(1,128)} %fb_ref.1, s32[1,8]{1,0:T(1,128)} %tm_ref.1, bf16[1,2048,128]{2,1,0:T(8,128)(2,1)} %sides_ref.1, bf16[1,128,1024]{2,1,0:T(8,128)(2,1)} %factor_ref.1, f32[128,256]{1,0:T(8,128)} %block_ref.1), custom_call_target="tpu_custom_call" | custom-call | tf_op jit(solution)/shard_map/pallas_call | solution.py:444
  71.4 0.0 copy-start
  71.4 1.9 %copy.9 = bf16[1,2048,128]{2,1,0:T(8,128)(2,1)} copy(bf16[1,2048,128]{2,1,0:T(8,128)(2,1)} %bitcast.1) | data formatting | bytes 1048576
  73.3 0.0 copy-done
  73.3 0.7 copy.10
Async XLA Ops:
  71.4 1.9 %copy-start = (f32[128,256]{1,0:T(8,128)S(1)}, f32[128,256]{1,0:T(8,128)}, u32[]{:S(2)}) copy-start(f32[128,256]{1,0:T(8,128)} %get-tuple-element.9) | copy-start | bytes 393220

commit v4 on v3

--- a/solution.py
+++ b/solution.py
@@ -12,8 +12,8 @@
 SLOTS = 256
 GROUPS = ((4, 3, 5, 2), (6, 1, 7, 0))
 SPLIT = 640
-A_PARTS = ((0, 320), (320, 320))
-B_PARTS = ((640, 192), (832, 192))
+A_PARTS = ((0, 352), (352, 352))
+B_PARTS = ((704, 160), (864, 160))
 MESH = pl.DeviceIdType.MESH
 BF16 = jnp.bfloat16
 F32 = jnp.float32

time: 74.1 us -> 74.7 us (level); the launches traced: 74 us -> 73.7 us
  no operation moved by 1% of the time
where the time goes in v4:
time: 74.7 us; the launch traced here: 73.7 us
  Pallas kernels  70.5 us (94%)
  local copies, waits for them, and re-layouts  2.56 us (3%)
    pallas_call x1, Pallas kernels, local(): pl.pallas_call(whole_kernel, out_shape=(shape(sides.shape, BF16), shape(i...  70.5 us
    unnamed x4, local copies, waits for them, and re-layouts  2.56 us

profile of v4, /device:TPU:1, one launch (start us, length us, event | category | flops | bytes accessed | tf_op | source)
XLA Modules:
  0.0 73.7 jit_solution(5411939992327718341)
XLA Ops:
  0.6 70.5 %shard_map.68 = (bf16[2048,128]{1,0:T(8,128)(2,1)}, f32[128,256]{1,0:T(8,128)}) custom-call(s32[1,8]{1,0:T(1,128)} %fb_ref.1, s32[1,8]{1,0:T(1,128)} %tm_ref.1, bf16[1,2048,128]{2,1,0:T(8,128)(2,1)} %sides_ref.1, bf16[1,128,1024]{2,1,0:T(8,128)(2,1)} %factor_ref.1, f32[128,256]{1,0:T(8,128)} %block_ref.1), custom_call_target="tpu_custom_call" | custom-call | tf_op jit(solution)/shard_map/pallas_call | solution.py:444
  71.2 0.0 copy-start
  71.2 1.9 %copy.9 = bf16[1,2048,128]{2,1,0:T(8,128)(2,1)} copy(bf16[1,2048,128]{2,1,0:T(8,128)(2,1)} %bitcast.1) | data formatting | bytes 1048576
  73.1 0.0 copy-done
  73.1 0.7 copy.10
Async XLA Ops:
  71.2 1.9 %copy-start = (f32[128,256]{1,0:T(8,128)S(1)}, f32[128,256]{1,0:T(8,128)}, u32[]{:S(2)}) copy-start(f32[128,256]{1,0:T(8,128)} %get-tuple-element.9) | copy-start | bytes 393220
